TPU v7x, 16 devices: a whole 2x2x2 slice. The times are simulated.
16 devices in a mesh: dz: 2 (over z), dy: 2 (over y), dx: 4 (over x, core).
Axes of the slice: x: 2, y: 2, z: 2, core: 2. Of those that a mesh axis runs over, the one named last changes fastest.
Arguments:
- x_tokens: bfloat16 [65536, 1024], P(('dz', 'dy', 'dx'))
- g_tokens: bfloat16 [65536, 1024], P(('dz', 'dy', 'dx'))
- w_one: bfloat16 [1024, 4096], replicated
- w_two: bfloat16 [4096, 1024], replicated
- w_three: bfloat16 [1024, 4096], replicated
- w_four: bfloat16 [4096, 1024], replicated
- clip_norm: float32 [1], replicated
Outputs:
- output 1: float32 [1024, 4096], replicated
- output 2: float32 [4096, 1024], replicated
- output 3: float32 [1024, 4096], replicated
- output 4: float32 [4096, 1024], replicated
- output 5: bfloat16 [65536, 1024], P(('dz', 'dy', 'dx'))
All inputs are finite; a program needn't handle non-finite values.
Results may differ from a plain program's by a relative error of at most 0.0114068.
Values are sent between devices in bfloat16 or wider.
A program may use at most 1 GiB of HBM per device.

v0:
```python
import jax
import jax.numpy as jnp
from jax import lax
from jax.sharding import PartitionSpec as P

BATCH_AXES = ('dz', 'dy', 'dx')
SCATTER_ORDER = ('dx', 'dy', 'dz')
GATHER_ORDER = ('dz', 'dy', 'dx')


def contract_rows(left, right):
    return lax.dot_general(left, right, (((0,), (0,)), ((), ())), preferred_element_type=jnp.float32)


def contract_cols(left, right):
    return lax.dot_general(left, right, (((1,), (1,)), ((), ())), preferred_element_type=jnp.float32)


def gelu_back(pre_act, upstream):
    gelu_out, gelu_pull = jax.vjp(jax.nn.gelu, pre_act.astype(jnp.float32))
    return gelu_pull(upstream.astype(jnp.float32))[0].astype(jnp.bfloat16)


def local_grads(x_rows, g_rows, w_one, w_two, w_three, w_four):
    a_one = jnp.dot(x_rows, w_one, preferred_element_type=jnp.float32).astype(jnp.bfloat16)
    h_one = jax.nn.gelu(a_one.astype(jnp.float32)).astype(jnp.bfloat16)
    h_two = (jnp.dot(h_one, w_two, preferred_element_type=jnp.float32) + x_rows.astype(jnp.float32)).astype(jnp.bfloat16)
    a_three = jnp.dot(h_two, w_three, preferred_element_type=jnp.float32).astype(jnp.bfloat16)
    h_three = jax.nn.gelu(a_three.astype(jnp.float32)).astype(jnp.bfloat16)
    grad_four = contract_rows(h_three, g_rows)
    dh_three = contract_cols(g_rows, w_four).astype(jnp.bfloat16)
    da_three = gelu_back(a_three, dh_three)
    grad_three = contract_rows(h_two, da_three)
    dh_two = (contract_cols(da_three, w_three) + g_rows.astype(jnp.float32)).astype(jnp.bfloat16)
    grad_two = contract_rows(h_one, dh_two)
    dh_one = contract_cols(dh_two, w_two).astype(jnp.bfloat16)
    da_one = gelu_back(a_one, dh_one)
    grad_one = contract_rows(x_rows, da_one)
    dx_rows = (contract_cols(da_one, w_one) + dh_two.astype(jnp.float32)).astype(jnp.bfloat16)
    return (grad_one, grad_two, grad_three, grad_four), dx_rows


def solution(mesh):
    device_count = mesh.shape['dz'] * mesh.shape['dy'] * mesh.shape['dx']
    row_spec = P(BATCH_AXES, None)

    def per_device(x_rows, g_rows, w_one, w_two, w_three, w_four, clip_norm):
        layer_grads, dx_rows = local_grads(x_rows, g_rows, w_one, w_two, w_three, w_four)
        grad_shards = []
        for layer_grad in layer_grads:
            flat_part = layer_grad.reshape(-1)
            for axis_name in SCATTER_ORDER:
                flat_part = lax.psum_scatter(flat_part, axis_name, scatter_dimension=0, tiled=True)
            grad_shards.append(flat_part / device_count)
        local_sq = sum(jnp.sum(shard_part * shard_part) for shard_part in grad_shards)
        total_sq = lax.psum(local_sq, BATCH_AXES)
        clip_scale = jnp.minimum(1.0, clip_norm[0] / jnp.sqrt(total_sq))
        clipped = []
        for shard_part, layer_grad in zip(grad_shards, layer_grads):
            flat_part = shard_part * clip_scale
            for axis_name in GATHER_ORDER:
                flat_part = lax.all_gather(flat_part, axis_name, axis=0, tiled=True)
            clipped.append(flat_part.reshape(layer_grad.shape))
        return tuple(clipped) + (dx_rows,)

    return jax.shard_map(per_device, mesh=mesh, in_specs=(row_spec, row_spec, P(), P(), P(), P(), P()), out_specs=(P(), P(), P(), P(), row_spec), check_vma=False)
```

profile of v0, /device:TPU:0, one launch (start us, length us, event | category | flops | bytes accessed | tf_op | source)
XLA Modules:
  0.0 3152.0 jit_solution(17332657899747628932)
XLA Ops:
  7.2 42.9 %convolution_convert_fusion.1 = bf16[4096,4096]{1,0:T(8,128)(2,1)} fusion(bf16[4096,1024]{1,0:T(8,128)(2,1)} %param.7, bf16[1024,4096]{1,0:T(8,128)(2,1)} %param.9), kind=kOutput, calls=%fused_computation.36 | convolution fusion | flops 34376515584 | bytes 50331648 | tf_op jit(solution)/shard_map/dot_general | solution.py:25
  50.1 50.1 %add_convert_fusion.2 = bf16[4096,1024]{1,0:T(8,128)(2,1)} fusion(bf16[4096,1024]{1,0:T(8,128)(2,1)} %param.7, bf16[4096,1024]{1,0:T(8,128)(2,1)} %param.10, bf16[4096,4096]{1,0:T(8,128)(2,1)} %convolution_convert_fusion.1), kind=kOutput, calls=%fused_computation.39 | convolution fusion | flops 34540093440 | bytes 58720256 | tf_op jit(solution)/shard_map/dot_general | solution.py:27
  100.3 43.2 %convolution_convert_fusion = bf16[4096,4096]{1,0:T(8,128)(2,1)} fusion(bf16[4096,1024]{1,0:T(8,128)(2,1)} %add_convert_fusion.2, bf16[1024,4096]{1,0:T(8,128)(2,1)} %param.11), kind=kOutput, calls=%fused_computation.35 | convolution fusion | flops 34376515584 | bytes 50331648 | tf_op jit(solution)/shard_map/dot_general | solution.py:28
  143.4 55.8 %fusion.24 = f32[512,8,8,128]{3,2,1,0:T(8,128)} fusion(bf16[4096,1024]{1,0:T(8,128)(2,1)} %param.8, bf16[4096,4096]{1,0:T(8,128)(2,1)} %convolution_convert_fusion), kind=kOutput, calls=%fused_computation.41 | convolution fusion | flops 34527510528 | bytes 58720256 | tf_op jit(solution)/shard_map/dot_general | solution.py:12
  199.2 76.7 %fusion.4 = bf16[4096,4096]{1,0:T(8,128)(2,1)} fusion(bf16[4096,4096]{1,0:T(8,128)(2,1)} %convolution_convert_fusion, bf16[4096,1024]{1,0:T(8,128)(2,1)} %param.8, bf16[4096,1024]{1,0:T(8,128)(2,1)S(1)} %copy-done.1), kind=kOutput, calls=%fused_computation.16 | convolution fusion | flops 34745614336 | bytes 83886080 | tf_op jit(solution)/shard_map/dot_general | solution.py:16
  276.0 43.1 %add_convert_fusion.1 = bf16[4096,1024]{1,0:T(8,128)(2,1)} fusion(bf16[4096,1024]{1,0:T(8,128)(2,1)} %param.8, bf16[4096,4096]{1,0:T(8,128)(2,1)} %fusion.4, bf16[1024,4096]{1,0:T(8,128)(2,1)} %param.11), kind=kOutput, calls=%fused_computation.38 | convolution fusion | flops 34372321280 | bytes 58720256 | tf_op jit(solution)/shard_map/dot_general | solution.py:16
  319.1 44.0 %convolution_bitcast_fusion.2 = f32[128,32,8,128]{3,2,1,0:T(8,128)} fusion(bf16[4096,1024]{1,0:T(8,128)(2,1)} %add_convert_fusion.2, bf16[4096,4096]{1,0:T(8,128)(2,1)} %fusion.4), kind=kOutput, calls=%fused_computation.43 | convolution fusion | flops 34359738368 | bytes 58720256 | tf_op jit(solution)/shard_map/dot_general | solution.py:12
  363.1 55.8 %convolution_bitcast_fusion.1 = f32[512,8,8,128]{3,2,1,0:T(8,128)} fusion(bf16[4096,1024]{1,0:T(8,128)(2,1)} %add_convert_fusion.1, bf16[4096,4096]{1,0:T(8,128)(2,1)} %convolution_convert_fusion.1), kind=kOutput, calls=%fused_computation.42 | convolution fusion | flops 34527510528 | bytes 58720256 | tf_op jit(solution)/shard_map/dot_general | solution.py:12
  418.9 76.7 %fusion.7 = bf16[4096,4096]{1,0:T(8,128)(2,1)} fusion(bf16[4096,4096]{1,0:T(8,128)(2,1)} %convolution_convert_fusion.1, bf16[4096,1024]{1,0:T(8,128)(2,1)} %add_convert_fusion.1, bf16[4096,1024]{1,0:T(8,128)(2,1)S(1)} %bitcast.45), kind=kOutput, calls=%fused_computation.19 | convolution fusion | flops 34745614336 | bytes 83886080 | tf_op jit(solution)/shard_map/dot_general | solution.py:16
  519.2 42.3 %convolution_bitcast_fusion = f32[1024,4096]{0,1:T(8,128)} fusion(bf16[4096,4096]{1,0:T(8,128)(2,1)} %fusion.7, bf16[4096,1024]{1,0:T(8,128)(2,1)S(1)} %bitcast.47), kind=kOutput, calls=%fused_computation.40 | convolution fusion | flops 34359738368 | bytes 58720256 | tf_op jit(solution)/shard_map/dot_general | solution.py:12
  561.5 17.4 copy.13
  605.3 1095.8 %all-reduce.19.cloned.1.call-done = (f32[4194304]{0:T(1024)}, f32[4194304]{0:T(1024)}, f32[4194304]{0:T(1024)}, f32[4194304]{0:T(1024)}) async-done(((f32[4194304]{0:T(1024)}, f32[4194304]{0:T(1024)}, f32[4194304]{0:T(1024)}, f32[4194304]{0:T(1024)}), (f32[4194304]{0:T(1024)}, f32[4194304]{0:T(1024)}, f32[4194304]{0:T(1024)}, f32[4194304]{0:T(1024)})) %all-reduce.19.cloned.1.call-update) | async-done | bytes 67108880
  1720.3 372.8 %all-reduce.21.cloned.1.call-done = (f32[1048576]{0:T(1024)}, f32[1048576]{0:T(1024)}, f32[1048576]{0:T(1024)}, f32[1048576]{0:T(1024)}) async-done(((f32[1048576]{0:T(1024)}, f32[1048576]{0:T(1024)}, f32[1048576]{0:T(1024)}, f32[1048576]{0:T(1024)}), (f32[1048576]{0:T(1024)}, f32[1048576]{0:T(1024)}, f32[1048576]{0:T(1024)}, f32[1048576]{0:T(1024)})) %all-reduce.21.cloned.1.call-update) | async-done | bytes 16777232
  2106.7 193.3 %all-reduce.23.cloned.1.call-done = (f32[524288]{0:T(1024)}, f32[524288]{0:T(1024)}, f32[524288]{0:T(1024)}, f32[524288]{0:T(1024)}) async-done(((f32[524288]{0:T(1024)}, f32[524288]{0:T(1024)}, f32[524288]{0:T(1024)}, f32[524288]{0:T(1024)}), (f32[524288]{0:T(1024)}, f32[524288]{0:T(1024)}, f32[524288]{0:T(1024)}, f32[524288]{0:T(1024)})) %all-reduce.23.cloned.1.call-update) | async-done | bytes 8388624
  2308.0 32.2 %psum.7 = f32[]{:T(128)} all-reduce(f32[]{:T(128)S(6)} %add.70), channel_id=1, replica_groups=mesh['dz'=2,'dy'=2,'dx'=4] {'dz','dy','dx'}, use_global_device_ids=true, to_apply=%region_16.0 | all-reduce | flops 1 | bytes 8 | tf_op jit(solution)/shard_map/psum | solution.py:56
  2350.3 25.0 all-gather.13.cloned.1.call-done
  2375.3 33.0 %all-gather.31.cloned.1.call-done = f32[524288]{0:T(1024)} async-done(((f32[262144]{0:T(1024)}), f32[524288]{0:T(1024)}) %all-gather.31.cloned.1.call-update) | async-done | bytes 2097168 | tf_op jit(solution)/shard_map/all_gather | solution.py:62
  2408.3 33.0 %all-gather.25.cloned.1.call-done = f32[524288]{0:T(1024)} async-done(((f32[262144]{0:T(1024)}), f32[524288]{0:T(1024)}) %all-gather.25.cloned.1.call-update) | async-done | bytes 2097168 | tf_op jit(solution)/shard_map/all_gather | solution.py:62
  2441.4 33.1 %all-gather.19.cloned.1.call-done = f32[524288]{0:T(1024)} async-done(((f32[262144]{0:T(1024)}), f32[524288]{0:T(1024)}) %all-gather.19.cloned.1.call-update) | async-done | bytes 2097168 | tf_op jit(solution)/shard_map/all_gather | solution.py:62
  2474.5 56.6 %all-gather.15.cloned.1.call-done = f32[1048576]{0:T(1024)} async-done(((f32[524288]{0:T(1024)}), f32[1048576]{0:T(1024)}) %all-gather.15.cloned.1.call-update) | async-done | bytes 4194320 | tf_op jit(solution)/shard_map/all_gather | solution.py:62
  2531.2 56.6 %all-gather.33.cloned.1.call-done = f32[1048576]{0:T(1024)} async-done(((f32[524288]{0:T(1024)}), f32[1048576]{0:T(1024)}) %all-gather.33.cloned.1.call-update) | async-done | bytes 4194320 | tf_op jit(solution)/shard_map/all_gather | solution.py:62
  2587.8 56.4 %all-gather.27.cloned.1.call-done = f32[1048576]{0:T(1024)} async-done(((f32[524288]{0:T(1024)}), f32[1048576]{0:T(1024)}) %all-gather.27.cloned.1.call-update) | async-done | bytes 4194320 | tf_op jit(solution)/shard_map/all_gather | solution.py:62
  2644.3 56.6 %all-gather.21.cloned.1.call-done = f32[1048576]{0:T(1024)} async-done(((f32[524288]{0:T(1024)}), f32[1048576]{0:T(1024)}) %all-gather.21.cloned.1.call-update) | async-done | bytes 4194320 | tf_op jit(solution)/shard_map/all_gather | solution.py:62
  2700.9 42.9 %add_convert_fusion = bf16[4096,1024]{1,0:T(8,128)(2,1)} fusion(bf16[4096,1024]{1,0:T(8,128)(2,1)} %add_convert_fusion.1, bf16[4096,4096]{1,0:T(8,128)(2,1)} %fusion.7, bf16[1024,4096]{1,0:T(8,128)(2,1)} %param.9), kind=kOutput, calls=%fused_computation.37 | convolution fusion | flops 34372321280 | bytes 58720256 | tf_op jit(solution)/shard_map/dot_general | solution.py:16
  2743.8 63.6 %all-gather.17.cloned.1.call-done = f32[4194304]{0:T(1024)} async-done(((f32[1048576]{0:T(1024)}), f32[4194304]{0:T(1024)}) %all-gather.17.cloned.1.call-update) | async-done | bytes 16777232 | tf_op jit(solution)/shard_map/all_gather | solution.py:62
  2807.4 18.2 reshape.38
  2825.6 88.5 %all-gather.35.cloned.1.call-done = f32[4194304]{0:T(1024)} async-done(((f32[1048576]{0:T(1024)}), f32[4194304]{0:T(1024)}) %all-gather.35.cloned.1.call-update) | async-done | bytes 16777232 | tf_op jit(solution)/shard_map/all_gather | solution.py:62
  2914.1 18.0 reshape.41
  2932.0 88.5 %all-gather.29.cloned.1.call-done = f32[4194304]{0:T(1024)} async-done(((f32[1048576]{0:T(1024)}), f32[4194304]{0:T(1024)}) %all-gather.29.cloned.1.call-update) | async-done | bytes 16777232 | tf_op jit(solution)/shard_map/all_gather | solution.py:62
  3020.6 18.2 reshape.40
  3038.8 88.3 %all-gather.23.cloned.1.call-done = f32[4194304]{0:T(1024)} async-done(((f32[1048576]{0:T(1024)}), f32[4194304]{0:T(1024)}) %all-gather.23.cloned.1.call-update) | async-done | bytes 16777232 | tf_op jit(solution)/shard_map/all_gather | solution.py:62
  3127.1 18.0 reshape.39
  (80 shorter events, 95.2 us)
Async XLA Ops:
  7.2 1694.0 %all-reduce.19.cloned.1.call-start = ((), (), s32[]{:S(2)}) async-start(), calls=%async_computation.12 | async-start | bytes 134217728
  143.4 55.8 %copy-start.1 = (bf16[4096,1024]{1,0:T(8,128)(2,1)S(1)}, bf16[4096,1024]{1,0:T(8,128)(2,1)}, u32[]{:S(2)}) copy-start(bf16[4096,1024]{1,0:T(8,128)(2,1)} %param.12) | copy-start | bytes 25165828
  319.1 99.8 %slice-start.4 = ((s8[8388608]{0:T(1024)(128)(4,1)}), s8[4194304]{0:T(1024)(128)(4,1)S(1)}, s32[]{:S(2)}) async-start(s8[8388608]{0:T(1024)(128)(4,1)} %bitcast.44), calls=%async_computation.19 | async-start | bytes 8388608
  363.1 55.8 %slice-start.5 = ((s8[8388608]{0:T(1024)(128)(4,1)}), s8[4194304]{0:T(1024)(128)(4,1)S(1)}, s32[]{:S(2)}) async-start(s8[8388608]{0:T(1024)(128)(4,1)} %bitcast.44), calls=%async_computation.20 | async-start | bytes 8388608
  495.6 16.3 copy-start
  495.6 23.6 slice-start.6
  511.9 7.3 slice-start.7
  579.0 15.6 slice-start
  579.0 15.6 slice-start.1
  579.0 15.6 slice-start.2
  579.0 16.5 slice-start.3
  603.4 0.7 copy-start.4
  603.4 1115.6 %copy-start.3 = (u32[16]{0:T(128)S(1)}, u32[16]{0:T(128)}, u32[]{:S(2)}) copy-start(u32[16]{0:T(128)} %constant.28) | copy-start | bytes 196
  603.5 1489.7 %all-reduce.21.cloned.1.call-start = ((), (), s32[]{:S(2)}) async-start(), calls=%async_computation.13 | async-start | bytes 33554432
  1705.6 399.8 %copy-start.2 = (u32[16]{0:T(128)S(1)}, u32[16]{0:T(128)}, u32[]{:S(2)}) copy-start(u32[16]{0:T(128)} %constant.32) | copy-start | bytes 196
  1719.0 580.9 %all-reduce.23.cloned.1.call-start = ((), (), s32[]{:S(2)}) async-start(), calls=%async_computation.14 | async-start | bytes 16777216
  2105.4 269.9 %all-gather.13.cloned.1.call-start = ((), (), s32[]{:S(2)}) async-start(), calls=%async_computation | async-start | bytes 3145728 | tf_op jit(solution)/shard_map/all_gather | solution.py:62
  2343.2 65.1 %all-gather.31.cloned.1.call-start = ((), (), s32[]{:S(2)}) async-start(), calls=%async_computation.9 | async-start | bytes 3145728 | tf_op jit(solution)/shard_map/all_gather | solution.py:62
  2345.5 95.7 %all-gather.25.cloned.1.call-start = ((), (), s32[]{:S(2)}) async-start(), calls=%async_computation.6 | async-start | bytes 3145728 | tf_op jit(solution)/shard_map/all_gather | solution.py:62
  2347.9 126.6 %all-gather.19.cloned.1.call-start = ((), (), s32[]{:S(2)}) async-start(), calls=%async_computation.3 | async-start | bytes 3145728 | tf_op jit(solution)/shard_map/all_gather | solution.py:62
  2350.2 180.9 %all-gather.15.cloned.1.call-start = ((), (), s32[]{:S(2)}) async-start(), calls=%async_computation.1 | async-start | bytes 6291456 | tf_op jit(solution)/shard_map/all_gather | solution.py:62
  2375.3 212.5 %all-gather.33.cloned.1.call-start = ((), (), s32[]{:S(2)}) async-start(), calls=%async_computation.10 | async-start | bytes 6291456 | tf_op jit(solution)/shard_map/all_gather | solution.py:62
  2408.3 236.0 %all-gather.27.cloned.1.call-start = ((), (), s32[]{:S(2)}) async-start(), calls=%async_computation.7 | async-start | bytes 6291456 | tf_op jit(solution)/shard_map/all_gather | solution.py:62
  2441.3 259.6 %all-gather.21.cloned.1.call-start = ((), (), s32[]{:S(2)}) async-start(), calls=%async_computation.4 | async-start | bytes 6291456 | tf_op jit(solution)/shard_map/all_gather | solution.py:62
  2474.5 332.9 %all-gather.17.cloned.1.call-start = ((), (), s32[]{:S(2)}) async-start(), calls=%async_computation.2 | async-start | bytes 20971520 | tf_op jit(solution)/shard_map/all_gather | solution.py:62
  2531.1 382.9 %all-gather.35.cloned.1.call-start = ((), (), s32[]{:S(2)}) async-start(), calls=%async_computation.11 | async-start | bytes 20971520 | tf_op jit(solution)/shard_map/all_gather | solution.py:62
  2587.8 432.8 %all-gather.29.cloned.1.call-start = ((), (), s32[]{:S(2)}) async-start(), calls=%async_computation.8 | async-start | bytes 20971520 | tf_op jit(solution)/shard_map/all_gather | solution.py:62
  2644.3 482.8 %all-gather.23.cloned.1.call-start = ((), (), s32[]{:S(2)}) async-start(), calls=%async_computation.5 | async-start | bytes 20971520 | tf_op jit(solution)/shard_map/all_gather | solution.py:62
Sparse Core Ops, SparseCore 0:
  603.6 1097.5 all-reduce.18
  1719.2 373.9 all-reduce.20
  2105.5 194.3 all-reduce.22
  2343.3 31.8 all-gather.12
  2377.2 31.0 all-gather.30
  2410.2 31.0 all-gather.24
  2443.4 31.0 all-gather.18
  2476.0 55.0 all-gather.14
  2532.6 55.0 all-gather.32
  2589.1 55.0 all-gather.26
  2645.8 55.0 all-gather.20
  2702.3 105.0 all-gather.16
  2808.9 105.0 all-gather.34
  2915.5 105.0 all-gather.28
  3022.0 105.0 all-gather.22
where the time goes:
time: 3160 us; the launch traced here: 3150 us
  waiting for transfers between devices  2340 us (74%)
  matrix products  574 us (18%)
  local copies, waits for them, and re-layouts  170 us (5%)
  blocking collectives  32.2 us (1%)
    unnamed x18, waiting for transfers between devices  1660 us
    all_gather x12, waiting for transfers between devices, per_device(): flat_part = lax.all_gather(flat_part, axis_name, axis=0, tiled=True)  679 us
    dot_general x4, matrix products, contract_cols(): lax.dot_general(left, right, (((1,), (1,)), ((), ())), preferred_element_...  239 us
    dot_general x4, matrix products, contract_rows(): lax.dot_general(left, right, (((0,), (0,)), ((), ())), preferred_element_...  198 us
    unnamed x41, local copies, waits for them, and re-layouts  80.2 us
    reshape x4, local copies, waits for them, and re-layouts, per_device(): clipped.append(flat_part.reshape(layer_grad.shape))  72.3 us
  transfers between devices with their start and end apart: 15, of which 15 were waited for; matrix products, arithmetic and copies ran while one was open for 3% of the time, Pallas kernels for 0%

commit v1 on v0

v1 whole, which is shorter than its diff:
```python
import functools
import math

import jax
import jax.numpy as jnp
from jax import lax
from jax.experimental import pallas as pl
from jax.experimental.pallas import tpu as pltpu
from jax.sharding import PartitionSpec as P

F32 = jnp.float32
BF16 = jnp.bfloat16
MESH = pl.DeviceIdType.MESH
AXES = ('dz', 'dy', 'dx')
ROOT = math.sqrt(2 / math.pi)
CUBE = ROOT * 0.044715

TOK = 4096
DM = 1024
DF = 4096
BC = 256
STEPS = DF // BC
BLOCKS = 2 * STEPS
MC = 1024
NCH = TOK // MC
EC = 32
NS = 6
ROWS = (DM, BC)
COLS = (BC, DM)


def nn(a, b):
    return jnp.dot(a, b, preferred_element_type=F32)


def nt(a, b):
    return lax.dot_general(a, b, (((1,), (1,)), ((), ())), preferred_element_type=F32)


def tn(a, b):
    return lax.dot_general(a, b, (((0,), (0,)), ((), ())), preferred_element_type=F32)


def gelu_pair(pre, up):
    x = pre.astype(F32)
    sq = x * x
    h = 0.5 * jnp.tanh(x * (ROOT + CUBE * sq)) + 0.5
    g = x * h
    slope = h + g * (1.0 - h) * (2 * ROOT + 6 * CUBE * sq)
    return g.astype(BF16), (up.astype(F32) * slope).astype(BF16)


def main_kernel(p0, p1, q0, wf0, wf1, wb0, wb1,
                ta, tb, dx_out, sq_out,
                pv, qv, acc, wf, wb, av, hv, gv, dv,
                own_a, own_b, r0a, r0b, r1a, r1b, r2a, r2b, r3a, r3b, sqv, sqr,
                ssem, rsem, lsem, wsem, psem, nsend, nrecv):
    own = (own_a, own_b)
    r0 = (r0a, r0b)
    r1 = (r1a, r1b)
    r2 = (r2a, r2b)
    r3 = (r3a, r3b)
    zb = lax.axis_index('dz')
    yb = lax.axis_index('dy')
    dxi = lax.axis_index('dx')
    xb = dxi // 2
    cb = dxi % 2
    partner = (zb, yb, 2 * xb + (1 - cb))

    def along(d):
        e0 = (1 - d) * (2 - d) // 2
        e1 = d * (2 - d)
        e2 = d * (d - 1) // 2
        bit = e0 * xb + e1 * yb + e2 * zb
        peer = (zb + e2 * (1 - 2 * zb), yb + e1 * (1 - 2 * yb), 2 * (xb + e0 * (1 - 2 * xb)) + cb)
        return bit, peer

    def route(i, u):
        d1 = (i + u + 2 * cb) % 3
        return along(d1), along((d1 + 1) % 3), along((d1 + 2) % 3)

    def remote(src, dst, stage, u, i, peer):
        s = i % NS
        return pltpu.make_async_remote_copy(
            src_ref=src, dst_ref=dst, send_sem=ssem.at[stage, u, s], recv_sem=rsem.at[stage, u, s],
            device_id=peer, device_id_type=MESH)

    def part(ref, slot, start, size):
        return ref.at[slot, pl.ds(pl.multiple_of(start, 16), size)]

    def load(ref, slot, start, size):
        return ref[slot, pl.ds(pl.multiple_of(start, 16), size), :]

    def region(u, i, start, size):
        ph = i // STEPS
        at = (i % STEPS) * BC
        if u == 0:
            return ta.at[ph, pl.ds(pl.multiple_of(start, 16), size), pl.ds(pl.multiple_of(at, BC), BC)]
        return tb.at[ph, pl.ds(pl.multiple_of(at + start, 16), size), :]

    def pair_copy(u, i):
        half = ROWS[u] // 2
        return remote(part(own[u], i % 2, (1 - cb) * half, half), r0[u].at[i % 3], 0, u, i, partner)

    def scatter_copy(k, u, i):
        (bits) = route(i, u)
        bit, peer = bits[k - 1]
        size = ROWS[u] // (2 << k)
        src = (r0, r1, r2)[k - 1][u]
        dst = (r1, r2, r3)[k - 1][u]
        slot = i % 3 if k == 1 else i % NS
        return remote(part(src, slot, (1 - bit) * size, size), dst.at[i % NS], k, u, i, peer)

    def offsets(u, i):
        (b1, _), (b2, _), (b3, _) = route(i, u)
        r = ROWS[u]
        oc = cb * (r // 2)
        o1 = oc + b1 * (r // 4)
        o2 = o1 + b2 * (r // 8)
        return oc, o1, o2, o2 + b3 * (r // 16)

    def gather_copy(k, u, i):
        oc, o1, o2, o3 = offsets(u, i)
        r = ROWS[u]
        way = route(i, u)
        if k == 4:
            return remote(r3[u].at[i % NS], region(u, i, o3, r // 16), k, u, i, way[2][1])
        start, size, peer = {5: (o2, r // 8, way[1][1]), 6: (o1, r // 4, way[0][1]), 7: (oc, r // 2, partner)}[k]
        return remote(region(u, i, start, size), region(u, i, start, size), k, u, i, peer)

    def keep_copy(u, i):
        o3 = offsets(u, i)[3]
        return pltpu.make_async_copy(r3[u].at[i % NS], region(u, i, o3, ROWS[u] // 16), lsem.at[u, i % NS])

    def h_pair(i):
        for u in range(2):
            pair_copy(u, i).start()

    def h_scatter1(i):
        for u in range(2):
            pair_copy(u, i).wait()
            half = ROWS[u] // 2
            r0[u][i % 3] += load(own[u], i % 2, cb * half, half)
            scatter_copy(1, u, i).start()

    def h_scatter(k, i):
        for u in range(2):
            scatter_copy(k - 1, u, i).wait()
            bit = route(i, u)[k - 2][0]
            size = ROWS[u] // (1 << k)
            src = (r0, r1)[k - 2][u]
            dst = (r1, r2)[k - 2][u]
            slot = i % 3 if k == 2 else i % NS
            dst[i % NS] += load(src, slot, bit * size, size)
            scatter_copy(k, u, i).start()

    def h_final(i):
        for u in range(2):
            scatter_copy(3, u, i).wait()
            bit = route(i, u)[2][0]
            size = ROWS[u] // 16
            tot = r3[u][i % NS] + load(r2[u], i % NS, bit * size, size)
            r3[u][i % NS] = tot
            t2 = jnp.square(tot * (1.0 / 16))
            s = jnp.zeros((8, 128), F32)
            for r in range(0, size, 8):
                for c in range(0, COLS[u], 128):
                    s = s + t2[r:r + 8, c:c + 128]
            sqv[0] += s
            keep_copy(u, i).start()
            gather_copy(4, u, i).start()

    def h_gather5(i):
        for u in range(2):
            keep_copy(u, i).wait()
            gather_copy(4, u, i).wait()
            gather_copy(5, u, i).start()

    def h_gather(k, i):
        for u in range(2):
            gather_copy(k - 1, u, i).wait()
            gather_copy(k, u, i).start()

    def h_done(i):
        for u in range(2):
            gather_copy(7, u, i).wait()

    plan = {
        0: [(3, functools.partial(h_scatter, 2)), (4, functools.partial(h_scatter, 3))],
        1: [(1, h_pair), (9, h_done), (8, functools.partial(h_gather, 7))],
        2: [(1, h_scatter1)],
        3: [(4, h_final), (5, h_gather5), (6, functools.partial(h_gather, 6))],
    }

    def hooks(g, c):
        for lag, fn in plan[c]:
            i = g - lag

            @pl.when(jnp.logical_and(i >= 0, i < BLOCKS))
            def _():
                fn(i)

    def wcopies(nxt, wf_hbm, wb_hbm):
        at = pl.multiple_of((nxt % STEPS) * BC, BC)
        return (pltpu.make_async_copy(wf_hbm.at[:, pl.ds(at, BC)], wf.at[nxt % 2], wsem.at[0, nxt % 2]),
                pltpu.make_async_copy(wb_hbm.at[pl.ds(at, BC), :], wb.at[nxt % 2], wsem.at[1, nxt % 2]))

    def wload(nxt):
        @pl.when(nxt < STEPS)
        def _():
            for cp in wcopies(nxt, wf0, wb0):
                cp.start()

        @pl.when(jnp.logical_and(nxt >= STEPS, nxt < BLOCKS))
        def _():
            for cp in wcopies(nxt, wf1, wb1):
                cp.start()

    def rows(c):
        return pl.ds(c * MC, MC)

    def dots(c, slot):
        av[c % 2] = nn(pv[rows(c), :], wf[slot]).astype(BF16)
        hv[c % 2] = nt(qv[rows(c), :], wb[slot]).astype(BF16)

    def elem(s):
        for k in range(MC // EC):
            rr = pl.ds(k * EC, EC)
            g, d = gelu_pair(av[s, rr, :], hv[s, rr, :])
            gv[s, rr, :] = g
            dv[s, rr, :] = d

    def grads(c, slot, bslot):
        s = c % 2
        b = tn(gv[s], qv[rows(c), :])
        a = tn(pv[rows(c), :], dv[s])
        if c == 0:
            own_b[bslot] = b
            own_a[bslot] = a
        else:
            own_b[bslot] += b
            own_a[bslot] += a
        acc[rows(c), :] += nt(dv[s], wf[slot])

    bar = pltpu.get_barrier_semaphore()
    for peer in (partner, along(0)[1], along(1)[1], along(2)[1]):
        pl.semaphore_signal(bar, inc=1, device_id=peer, device_id_type=MESH)
    pl.semaphore_wait(bar, 4)

    wload(0)
    pcopy = pltpu.make_async_copy(p0, pv, psem.at[0])
    qcopy = pltpu.make_async_copy(q0, qv, psem.at[1])
    pcopy.start()
    qcopy.start()
    sqv[...] = jnp.zeros(sqv.shape, F32)
    pcopy.wait()
    qcopy.wait()

    def acc_init(k, _):
        rr = pl.ds(pl.multiple_of(k * 128, 128), 128)
        acc[rr, :] = qv[rr, :].astype(F32)
        return 0

    lax.fori_loop(0, TOK // 128, acc_init, 0)

    def phase(ph, _):
        zero = jnp.zeros((MC, BC), BF16)
        av[1] = zero
        hv[1] = zero
        gv[0] = zero
        dv[0] = zero

        def step(j, _):
            g = ph * STEPS + j
            slot = g % 2
            for cp in wcopies(g, wf0, wb0):
                cp.wait()
            for c in range(NCH):
                dots(c, slot)
                elem((c + 1) % 2)
                if c < 2:
                    grads(c + 2, 1 - slot, 1 - slot)
                else:
                    grads(c - 2, slot, slot)
                if c == 1:
                    wload(g + 1)
                hooks(g, c)
            return 0

        lax.fori_loop(0, STEPS, step, 0)
        elem(1)
        grads(2, 1, 1)
        grads(3, 1, 1)

        @pl.when(ph == 0)
        def _():
            cp = pltpu.make_async_copy(p1, pv, psem.at[0])
            cp.start()

            def turn(k, _):
                rr = pl.ds(pl.multiple_of(k * 128, 128), 128)
                q = acc[rr, :].astype(BF16)
                qv[rr, :] = q
                acc[rr, :] = q.astype(F32)
                return 0

            lax.fori_loop(0, TOK // 128, turn, 0)
            cp.wait()

        @pl.when(ph == 1)
        def _():
            def turn(k, _):
                rr = pl.ds(pl.multiple_of(k * 128, 128), 128)
                qv[rr, :] = acc[rr, :].astype(BF16)
                return 0

            lax.fori_loop(0, TOK // 128, turn, 0)
            pltpu.make_async_copy(qv, dx_out, psem.at[1]).start()

        return 0

    lax.fori_loop(0, 2, phase, 0)

    def drain(g, _):
        for c in range(NCH):
            hooks(g, c)
        return 0

    lax.fori_loop(BLOCKS, BLOCKS + 10, drain, 0)

    for k, peer in enumerate((partner, along(0)[1], along(1)[1], along(2)[1])):
        cp = pltpu.make_async_remote_copy(
            src_ref=sqv.at[k], dst_ref=sqr.at[k], send_sem=nsend.at[k], recv_sem=nrecv.at[k],
            device_id=peer, device_id_type=MESH)
        cp.start()
        cp.wait()
        sqv[k + 1] = sqv[k] + sqr[k]
    sq_out[...] = sqv[4]
    pltpu.make_async_copy(qv, dx_out, psem.at[1]).wait()


def run_main(h_two, x_rows, g_rows, w_one, w_two, w_three, w_four):
    vm = pltpu.VMEM
    dma = pltpu.SemaphoreType.DMA
    scratch = [
        vm((TOK, DM), BF16), vm((TOK, DM), BF16), vm((TOK, DM), F32),
        vm((2, DM, BC), BF16), vm((2, BC, DM), BF16),
        vm((2, MC, BC), BF16), vm((2, MC, BC), BF16), vm((2, MC, BC), BF16), vm((2, MC, BC), BF16),
        vm((2, DM, BC), F32), vm((2, BC, DM), F32),
    ]
    for k, slots in ((2, 3), (4, NS), (8, NS), (16, NS)):
        scratch += [vm((slots, ROWS[u] // k, COLS[u]), F32) for u in range(2)]
    scratch += [vm((5, 8, 128), F32), vm((4, 8, 128), F32),
                dma((8, 2, NS)), dma((8, 2, NS)), dma((2, NS)), dma((2, 2)), dma((2,)), dma((4,)), dma((4,))]
    hbm = pl.BlockSpec(memory_space=pl.ANY)
    flops = 2 * 10 * TOK * DM * DF
    return pl.pallas_call(
        main_kernel,
        out_shape=(jax.ShapeDtypeStruct((2, DM, DF), F32), jax.ShapeDtypeStruct((2, DF, DM), F32),
                   jax.ShapeDtypeStruct((TOK, DM), BF16), jax.ShapeDtypeStruct((8, 128), F32)),
        in_specs=[hbm] * 7,
        out_specs=(hbm, hbm, hbm, pl.BlockSpec(memory_space=pltpu.VMEM)),
        scratch_shapes=scratch,
        compiler_params=pltpu.CompilerParams(
            collective_id=0, has_side_effects=True, vmem_limit_bytes=63 * 2 ** 20),
        cost_estimate=pl.CostEstimate(flops=flops, bytes_accessed=200_000_000, transcendentals=2 * TOK * DF),
        name='grad_main',
    )(h_two, x_rows, g_rows, w_three, w_one, w_four, w_two)


def solution(mesh):
    row_spec = P(AXES, None)

    def per_device(x_rows, g_rows, w_one, w_two, w_three, w_four, clip_norm):
        a_one = nn(x_rows, w_one).astype(BF16)
        h_one = jax.nn.gelu(a_one.astype(F32)).astype(BF16)
        h_two = (nn(h_one, w_two) + x_rows.astype(F32)).astype(BF16)
        ta, tb, dx_rows, sq = run_main(h_two, x_rows, g_rows, w_one, w_two, w_three, w_four)
        scale = jnp.minimum(1.0, clip_norm[0] / jnp.sqrt(jnp.sum(sq)))
        return tuple(part * (1.0 / 16) * scale for part in (ta[1], tb[1], ta[0], tb[0])) + (dx_rows,)

    return jax.shard_map(per_device, mesh=mesh, in_specs=(row_spec, row_spec, P(), P(), P(), P(), P()),
                         out_specs=(P(), P(), P(), P(), row_spec), check_vma=False)
```

time: 3160 us -> 744 us (0.24)
  waiting for transfers between devices: 2340 us -> 0 us
  Pallas kernels: 0 us -> 572 us
  matrix products: 574 us -> 116 us
  local copies, waits for them, and re-layouts: 170 us -> 7.76 us
  blocking collectives: 32.2 us -> 0 us
    unnamed x18 -> x0, waiting for transfers between devices: 1660 us -> none
    all_gather x12 -> x0, waiting for transfers between devices: 679 us -> none  [per_device(): flat_part = lax.all_gather(flat_part, axis_name, axis=0, tiled=True)]
    pallas_call x0 -> x1, Pallas kernels: none -> 572 us  [run_main(): pl.pallas_call(main_kernel, out_shape=(jax.ShapeDtypeStruct((2, DM, DF),...]
    dot_general x11 -> x2, matrix products: 574 us -> 116 us  [nn(): return jnp.dot(a, b, preferred_element_type=F32)]
    unnamed x41 -> x1, local copies, waits for them, and re-layouts: 80.2 us -> 7.76 us
    reshape x4 -> x0, local copies, waits for them, and re-layouts: 72.3 us -> none  [per_device(): clipped.append(flat_part.reshape(layer_grad.shape))]
    mul x4 -> x2, other arithmetic: 9.07 us -> 43.6 us  [per_device(): part * (1.0 / 16) * scale]
    psum x1 -> x0, blocking collectives: 32.2 us -> none  [per_device(): total_sq = lax.psum(local_sq, BATCH_AXES)]
  transfers between devices with their start and end apart: 15 -> 0, of which waited for: 15 -> 0; matrix products, arithmetic and copies ran while one was open for 3% -> 0% of each run, Pallas kernels for 0% -> 0%
where the time goes in v1:
time: 744 us; the launch traced here: 743 us
  Pallas kernels  572 us (77%)
  matrix products  116 us (16%)
  other arithmetic  44.9 us (6%)
  local copies, waits for them, and re-layouts  7.76 us (1%)
    pallas_call x1, Pallas kernels, run_main(): pl.pallas_call(main_kernel, out_shape=(jax.ShapeDtypeStruct((2, DM, DF),...  572 us
    dot_general x2, matrix products, nn(): return jnp.dot(a, b, preferred_element_type=F32)  116 us
    mul x2, other arithmetic, per_device(): part * (1.0 / 16) * scale  43.6 us

profile of v1, /device:TPU:0, one launch (start us, length us, event | category | flops | bytes accessed | tf_op | source)
XLA Modules:
  0.0 742.9 jit_solution(3085823582177000470)
XLA Ops:
  1.3 72.9 %fusion.28 = bf16[4096,4096]{1,0:T(8,128)(2,1)} fusion(bf16[4096,1024]{1,0:T(8,128)(2,1)} %p1.1, bf16[1024,4096]{1,0:T(8,128)(2,1)} %wf1.1), kind=kOutput, calls=%fused_computation.9.clone.clone.clone.clone.1 | convolution fusion | flops 34544287744 | bytes 50331648 | tf_op jit(solution)/shard_map/dot_general | solution.py:33
  74.2 42.7 %add_convert_fusion.p0 = bf16[4096,1024]{1,0:T(8,128)(2,1)} fusion(bf16[4096,1024]{1,0:T(8,128)(2,1)} %p1.1, bf16[4096,1024]{1,0:T(8,128)(2,1)} %wb1.1, bf16[4096,4096]{1,0:T(8,128)(2,1)} %fusion.28), kind=kOutput, calls=%fused_computation.15 | convolution fusion | flops 34372321280 | bytes 58720256 | tf_op jit(solution)/shard_map/dot_general | solution.py:33
  116.9 572.2 %grad_main.1 = (f32[2,1024,4096]{2,1,0:T(8,128)}, f32[2,4096,1024]{2,1,0:T(8,128)}, bf16[4096,1024]{1,0:T(8,128)(2,1)}, f32[8,128]{1,0:T(8,128)}) custom-call(bf16[4096,1024]{1,0:T(8,128)(2,1)} %add_convert_fusion.p0, bf16[4096,1024]{1,0:T(8,128)(2,1)} %p1.1, bf16[4096,1024]{1,0:T(8,128)(2,1)} %q0.1, bf16[1024,4096]{1,0:T(8,128)(2,1)} %wf0.1, ...), custom_call_target="tpu_custom_call" | custom-call | flops 343597383680 | bytes 200000000 | tf_op jit(solution)/shard_map/grad_main/pallas_call | solution.py:357
  689.2 1.3 reduce_sum.9
  691.2 21.3 %multiply_bitcast_fusion.1 = (f32[1024,4096]{1,0:T(8,128)}, f32[1024,4096]{1,0:T(8,128)}) fusion(f32[2,1024,4096]{2,1,0:T(8,128)} %get-tuple-element.9, f32[]{:T(128)S(6)} %mul.66), kind=kLoop, calls=%fused_computation.12 | loop fusion | flops 8388608 | bytes 67108864 | tf_op jit(solution)/shard_map/mul | solution.py:380
  712.4 22.3 %multiply_bitcast_fusion = (f32[4096,1024]{1,0:T(8,128)}, f32[4096,1024]{1,0:T(8,128)}) fusion(f32[2,4096,1024]{2,1,0:T(8,128)} %get-tuple-element.11, f32[]{:T(128)S(6)} %mul.66), kind=kLoop, calls=%fused_computation.11 | loop fusion | flops 8388608 | bytes 67108864 | tf_op jit(solution)/shard_map/mul | solution.py:380
  734.8 7.8 %copy.14 = bf16[4096,1024]{1,0:T(8,128)(2,1)} copy(bf16[4096,1024]{1,0:T(8,128)(2,1)} %get-tuple-element.26) | data formatting | bytes 16777216
